TPU v7x, 32 devices: a whole 2x2x4 slice. The times are simulated.
32 devices in a mesh: ta: 4 (over z), sa: 8 (over y, x, core).
Axes of the slice: x: 2, y: 2, z: 4, core: 2. Of those that a mesh axis runs over, the one named last changes fastest.
Arguments:
- frames: float32 [16, 8, 512, 4096], P('ta', 'sa'), may hold values from -6 to 6
- taps: float32 [7], replicated, may hold values from 0.1 to 0.3
Outputs:
- columns: float32 [64, 16, 512, 512], P('sa', 'ta')
All inputs are finite; a program needn't handle non-finite values.
Results may differ from a plain program's by a relative error of at most 0.00002.
Values sent between devices are 32-bit elements; how exact they have to be, the bound alone decides.
A program may use at most 256 MiB of HBM per device.

v0:
```python
import jax
import jax.numpy as jnp
from jax import lax
from jax.sharding import PartitionSpec as P

TS = 512


def extended_2(cells, sides, width):
    for axis, dim in sides:
        count = lax.axis_size(axis)
        ends = count - 1
        head = lax.slice_in_dim(cells, 0, width, axis=dim)
        tail = lax.slice_in_dim(cells, cells.shape[dim] - width, cells.shape[dim], axis=dim)
        cells = jnp.concatenate(
            [
                lax.ppermute(tail, axis, [(i, (i + 1) % count) for i in range(ends)]),
                cells,
                lax.ppermute(head, axis, [((i + 1) % count, i) for i in range(ends)]),
            ],
            axis=dim,
        )
    return cells


def pack_tiles(block, readers):
    count = block.shape[0]
    per_tile = TS // readers
    tile_rows = block.shape[2] // per_tile
    tile_cols = block.shape[3] // TS
    shaped = block.reshape(count, tile_rows, per_tile, tile_cols, TS)
    return shaped.transpose(1, 3, 0, 2, 4).reshape(tile_rows * tile_cols, 1, count, per_tile, TS)


def unpack_tiles(received):
    owned = received.shape[0]
    count = received.shape[2]
    return received.transpose(0, 2, 3, 1, 4).reshape(owned, count, TS, TS)


def on_device(frames, taps):
    steps = frames.shape[0]
    readers = lax.axis_size("sa")
    received = lax.all_to_all(
        pack_tiles(frames, readers), "sa", split_axis=0, concat_axis=1, tiled=True
    )
    tiles = unpack_tiles(received)
    extended = extended_2(tiles, (("ta", 1),), 3)
    total = jnp.zeros((extended.shape[0], steps, TS, TS), jnp.float32)
    for offset in range(7):
        total = total + taps[offset] * extended[:, offset : offset + steps]
    return total


def solution(mesh):
    placed = (P("ta", "sa", None, None), P())
    return jax.shard_map(
        on_device, mesh=mesh, in_specs=placed, out_specs=P("sa", "ta", None, None), check_vma=False
    )
```

profile of v0, /device:TPU:0, one launch (start us, length us, event | category | flops | bytes accessed | tf_op | source)
XLA Modules:
  0.0 1142.3 jit_solution(14448742951515873485)
XLA Ops:
  0.0 38.0 %copy.8 = f32[256,8,8,512]{3,2,1,0:T(8,128)} copy(f32[256,8,8,512]{3,1,2,0:T(8,128)} %bitcast.32) | data formatting | bytes 67108864
  38.0 28.2 %copy.5 = f32[8,8,4,64,512]{4,3,2,1,0:T(8,128)S(1)} copy(f32[8,8,4,64,512]{4,1,3,0,2:T(8,128)} %bitcast.31) | data formatting | bytes 67108864 | tf_op jit(solution)/shard_map/transpose | solution.py:32
  66.3 369.0 %all_to_all.18 = f32[64,1,4,64,512]{4,3,2,1,0:T(8,128)} all-to-all(f32[64,1,4,64,512]{4,3,2,1,0:T(8,128)S(1)} %bitcast.29), channel_id=1, replica_groups=mesh['ta'=4,'sa'=8] {'sa'}, dimensions={0} | all-to-all | bytes 67108864 | tf_op jit(solution)/shard_map/all_to_all | solution.py:44
  435.2 31.8 %copy.10 = f32[8,4,64,8,512]{4,3,2,1,0:T(8,128)} copy(f32[8,4,64,8,512]{4,2,1,0,3:T(8,128)} %bitcast.30) | data formatting | bytes 67108864 | tf_op jit(solution)/shard_map/transpose | solution.py:38
  467.0 0.0 copy-start
  467.0 32.0 %fusion.16 = (f32[8,3,512,512]{3,2,1,0:T(8,128)}, f32[8,3,512,512]{3,2,1,0:T(8,128)}) fusion(f32[8,4,512,512]{3,2,1,0:T(8,128)} %bitcast.27), kind=kLoop, calls=%fused_computation.27 | loop fusion | bytes 100663296 | tf_op jit(solution)/shard_map/slice | solution.py:14
  498.9 12.5 %collective-permute-start = (f32[8,3,512,512]{3,2,1,0:T(8,128)}, f32[8,3,512,512]{3,2,1,0:T(8,128)}, u32[]{:S(2)}, u32[]{:S(2)}) collective-permute-start(f32[8,3,512,512]{3,2,1,0:T(8,128)} %get-tuple-element.5), channel_id=1, source_target_pairs={{0,8},{8,16},{16,24},{1,9},{9,17},{17,25},{2,10},{10,18},{18,26},{... | collective-permute-start | bytes 75497480 | tf_op jit(solution)/shard_map/ppermute | solution.py:17
  511.4 1.3 collective-permute-start.1
  512.7 0.0 copy-done
  512.7 0.7 fusion.17
  513.4 528.7 %collective-permute-done = f32[8,3,512,512]{3,2,1,0:T(8,128)} collective-permute-done((f32[8,3,512,512]{3,2,1,0:T(8,128)}, f32[8,3,512,512]{3,2,1,0:T(8,128)}, u32[]{:S(2)}, u32[]{:S(2)}) %collective-permute-start) | collective-permute-done | bytes 25165856 | tf_op jit(solution)/shard_map/ppermute | solution.py:17
  1042.1 12.4 %collective-permute-done.1 = f32[8,3,512,512]{3,2,1,0:T(8,128)} collective-permute-done((f32[8,3,512,512]{3,2,1,0:T(8,128)}, f32[8,3,512,512]{3,2,1,0:T(8,128)}, u32[]{:S(2)}, u32[]{:S(2)}) %collective-permute-start.1) | collective-permute-done | bytes 25165856 | tf_op jit(solution)/shard_map/ppermute | solution.py:19
  1054.5 87.8 %fusion.3 = f32[8,4,512,512]{3,2,1,0:T(8,128)} fusion(f32[8,4,512,512]{3,2,1,0:T(8,128)} %bitcast.28, f32[8,3,512,512]{3,2,1,0:T(8,128)} %collective-permute-done.1, f32[8,3,512,512]{3,2,1,0:T(8,128)} %collective-permute-done, f32[]{:T(128)} %bitcast.14, f32[]{:T(128)} %bitcast.13, f32[]{:T(128)} %bitcast.12, f32[]{:T(128)} %bitcast.11, f32[]{:T(128)} %bitcast.10, ...), kind=kLoop, calls=%fused_computation.11 | loop fusion | flops 159383552 | bytes 117440544 | tf_op jit(solution)/shard_map/add | solution.py:51
Async XLA Ops:
  467.0 45.7 %copy-start = (f32[7]{0:T(128)S(1)}, f32[7]{0:T(128)}, u32[]{:S(2)}) copy-start(f32[7]{0:T(128)} %param.3) | copy-start | bytes 88
  498.9 543.1 %collective-permute-start = (f32[8,3,512,512]{3,2,1,0:T(8,128)}, f32[8,3,512,512]{3,2,1,0:T(8,128)}, u32[]{:S(2)}, u32[]{:S(2)}) collective-permute-start(f32[8,3,512,512]{3,2,1,0:T(8,128)} %get-tuple-element.5), channel_id=1, source_target_pairs={{0,8},{8,16},{16,24},{1,9},{9,17},{17,25},{2,10},{10,18},{18,26},{... | collective-permute-start | bytes 75497480 | tf_op jit(solution)/shard_map/ppermute | solution.py:17
  511.4 543.1 %collective-permute-start.1 = (f32[8,3,512,512]{3,2,1,0:T(8,128)}, f32[8,3,512,512]{3,2,1,0:T(8,128)}, u32[]{:S(2)}, u32[]{:S(2)}) collective-permute-start(f32[8,3,512,512]{3,2,1,0:T(8,128)} %get-tuple-element.6), channel_id=1, source_target_pairs={{8,0},{16,8},{24,16},{9,1},{17,9},{25,17},{10,2},{18,10},{26,18},{... | collective-permute-start | bytes 75497480 | tf_op jit(solution)/shard_map/ppermute | solution.py:19
where the time goes:
time: 1140 us
  waiting for transfers between devices  541 us (47%)
  blocking collectives  369 us (32%)
  local copies, waits for them, and re-layouts  131 us (11%)
  other arithmetic  87.8 us (8%)
  starting transfers between devices  13.7 us (1%)
    ppermute x1, waiting for transfers between devices, extended_2(): lax.ppermute(tail, axis, [(i, (i + 1) % count) for i in range(ends)])  529 us
    all_to_all x1, blocking collectives, on_device(): lax.all_to_all(pack_tiles(frames, readers), 'sa', split_axis=0, concat_ax...  369 us
    add x1, other arithmetic, on_device(): total = total + taps[offset] * extended[:, offset:offset + steps]  87.8 us
    unnamed x3, local copies, waits for them, and re-layouts  38 us
    slice x1, local copies, waits for them, and re-layouts, extended_2(): lax.slice_in_dim(cells, cells.shape[dim] - width, cells.shape[dim], axis=...  32 us
    transpose x1, local copies, waits for them, and re-layouts, unpack_tiles(): return received.transpose(0, 2, 3, 1, 4).reshape(owned, count, TS, TS)  31.8 us
    transpose x1, local copies, waits for them, and re-layouts, pack_tiles(): shaped.transpose(1, 3, 0, 2, 4)  28.2 us
  transfers between devices with their start and end apart: 2, of which 2 were waited for; matrix products, arithmetic and copies ran while one was open for 0% of the time, Pallas kernels for 0%

commit v1 on v0

v1 whole, which is shorter than its diff:
```python
import functools

import jax
import jax.numpy as jnp
from jax import lax
from jax.experimental import pallas as pl
from jax.experimental.pallas import tpu as pltpu
from jax.sharding import PartitionSpec as P

TS = 512
REACH = 3
LATE = 1


def partner(me, m, n, sign):
    if n & (n - 1):
        return (me + sign * m + n) % n
    other, bit = me, 1
    while bit < n:
        if m & bit:
            other = other + bit * (1 - 2 * ((me // bit) % 2))
        bit *= 2
    return other


def exchange_kernel(groups, n, rows, width, sent, frames, stage, low, high, own, own_sem,
                    a_send, a_recv, up_send, up_recv, down_send, down_recv):
    steps = frames.shape[0]
    group, me = lax.axis_index("ta"), lax.axis_index("sa")
    across = frames.shape[3] // width
    order = sorted(range(1, n), key=lambda m: (bin(m >> 1).count("1"), m & 1, m))
    has_prev, has_next = group > 0, group < groups - 1

    def block_for(owner):
        row = pl.ds(pl.multiple_of((owner // across) * rows, 8), rows)
        if across == 1:
            return frames.at[:, 0, row, :]
        return frames.at[:, 0, row, pl.ds(pl.multiple_of((owner % across) * width, TS), width)]

    barrier = pltpu.get_barrier_semaphore()
    for m in order:
        pl.semaphore_signal(barrier, inc=1, device_id={"sa": partner(me, m, n, 1)})

    @pl.when(has_prev)
    def _():
        pl.semaphore_signal(barrier, inc=1, device_id={"ta": group - 1})

    @pl.when(has_next)
    def _():
        pl.semaphore_signal(barrier, inc=1, device_id={"ta": group + 1})

    def block_copy(m):
        return pltpu.make_async_remote_copy(
            src_ref=block_for(partner(me, m, n, 1)), dst_ref=stage.at[me],
            send_sem=a_send.at[m], recv_sem=a_recv.at[m], device_id={"sa": partner(me, m, n, 1)})

    def edge_copy(m, which):
        source = partner(me, m, n, -1)
        if m == 0:
            row = pl.ds(pl.multiple_of((me // across) * rows, 8), rows)
            col = pl.ds(pl.multiple_of((me % across) * width, TS), sent)
            tail = frames.at[pl.ds(steps - REACH, REACH), 0, row, col]
            head = frames.at[pl.ds(0, REACH), 0, row, col]
        else:
            tail = stage.at[source, pl.ds(steps - REACH, REACH), :, pl.ds(0, sent)]
            head = stage.at[source, pl.ds(0, REACH), :, pl.ds(0, sent)]
        if which == "up":
            return pltpu.make_async_remote_copy(
                src_ref=tail, dst_ref=low.at[source],
                send_sem=up_send.at[m], recv_sem=up_recv.at[m], device_id={"ta": group + 1})
        return pltpu.make_async_remote_copy(
            src_ref=head, dst_ref=high.at[source],
            send_sem=down_send.at[m], recv_sem=down_recv.at[m], device_id={"ta": group - 1})

    def send_edges(m):
        @pl.when(has_next)
        def _():
            edge_copy(m, "up").start()

        @pl.when(has_prev)
        def _():
            edge_copy(m, "down").start()

    load = pltpu.make_async_copy(block_for(me), own, own_sem.at[0])
    load.start()

    neighbours = jnp.where(has_prev, 1, 0) + jnp.where(has_next, 1, 0)
    pl.semaphore_wait(barrier, n - 1 + neighbours)

    send_edges(0)
    for m in order:
        block_copy(m).start()
    load.wait()
    store = pltpu.make_async_copy(own, stage.at[me], own_sem.at[1])
    store.start()
    for m in order:
        block_copy(m).wait_recv()
        send_edges(m)
    store.wait()
    for m in order:
        block_copy(m).wait_send()
    for m in [0] + order:
        @pl.when(has_next)
        def _():
            edge_copy(m, "up").wait_send()
            edge_copy(m, "down").wait_recv()

        @pl.when(has_prev)
        def _():
            edge_copy(m, "down").wait_send()
            edge_copy(m, "up").wait_recv()


def exchanged(frames, groups, n, rows, width, sent):
    steps = frames.shape[0]
    any_space = pl.BlockSpec(memory_space=pl.ANY)
    edge = jax.ShapeDtypeStruct((n, REACH, rows, sent), jnp.float32)
    dma = pltpu.SemaphoreType.DMA((n,))
    return pl.pallas_call(
        functools.partial(exchange_kernel, groups, n, rows, width, sent),
        out_shape=[jax.ShapeDtypeStruct((n, steps, rows, width), jnp.float32), edge, edge],
        in_specs=[any_space],
        out_specs=[any_space] * 3,
        scratch_shapes=[pltpu.VMEM((steps, rows, width), jnp.float32), pltpu.SemaphoreType.DMA((2,)),
                        dma, dma, dma, dma, dma, dma],
        compiler_params=pltpu.CompilerParams(collective_id=0, has_side_effects=True),
        name="exchange",
    )(frames)


def smooth_kernel(groups, taps, stage, low, high, *rest):
    out, woven = rest[-2:]
    n, steps, rows, cols = stage.shape
    group = lax.axis_index("ta")
    first, last = group == 0, group == groups - 1
    weights = [taps[j] for j in range(2 * REACH + 1)]

    for c in range(0, cols, 128):
        lanes = pl.ds(c, 128)

        def one_source(s, carry):
            for r in range(0, rows, 8):
                at = (pl.ds(r, 8), lanes)
                lo = [jnp.where(first, 0.0, low[(s, j) + at]) for j in range(REACH)]
                hi = [jnp.where(last, 0.0, high[(s, j) + at]) for j in range(REACH)]
                cells = lo + [stage[(s, t) + at] for t in range(steps)] + hi
                for t in range(steps):
                    total = weights[0] * cells[t]
                    for j in range(1, 2 * REACH + 1):
                        total = total + weights[j] * cells[t + j]
                    woven[t, pl.ds(r * n + s, 8, stride=n), :] = total
            return carry

        lax.fori_loop(0, n, one_source, 0)
        for t in range(steps):
            out[t, :, lanes] = woven[t]


def smoothed(taps, stage, low, high, groups, start, count, col_tiles, edge_start, owned, into=None):
    n, steps, rows, _ = stage.shape
    per_tile = TS // n
    height = min(per_tile, max(8, 256 // n))
    splits = per_tile // height

    def source_map(shift):
        return lambda k, h: (0, 0, ((k + start) // col_tiles) * splits + h, (k + start) % col_tiles - shift)

    specs = [
        pl.BlockSpec(memory_space=pltpu.SMEM),
        pl.BlockSpec((n, steps, height, TS), source_map(0)),
        pl.BlockSpec((n, REACH, height, TS), source_map(edge_start)),
        pl.BlockSpec((n, REACH, height, TS), source_map(edge_start)),
    ]
    operands = [taps, stage, low, high]
    if into is not None:
        specs.append(pl.BlockSpec(memory_space=pl.ANY))
        operands.append(into)
    moved = count * steps * TS * TS * 4
    return pl.pallas_call(
        functools.partial(smooth_kernel, groups),
        grid=(count, splits),
        out_shape=jax.ShapeDtypeStruct((owned, steps, TS, TS), jnp.float32),
        in_specs=specs,
        out_specs=pl.BlockSpec((None, steps, height * n, TS), lambda k, h: (k + start, 0, h, 0)),
        scratch_shapes=[pltpu.VMEM((steps, height * n, 128), jnp.float32)],
        input_output_aliases={} if into is None else {4: 0},
        compiler_params=pltpu.CompilerParams(vmem_limit_bytes=60 * 1024 * 1024),
        cost_estimate=pl.CostEstimate(flops=moved * 4, bytes_accessed=moved * 7 // 2, transcendentals=0),
        name="smooth",
    )(*operands)


def on_device(frames, taps):
    groups, n = lax.axis_size("ta"), lax.axis_size("sa")
    tile_rows, tile_cols = frames.shape[2] * n // TS, frames.shape[3] // TS
    owned = tile_rows * tile_cols // n
    col_tiles = min(owned, tile_cols)
    width = col_tiles * TS
    rows = max(1, owned // tile_cols) * (TS // n)
    late = LATE if owned == col_tiles and col_tiles > LATE else 0
    sent = width - late * TS
    stage, low, high = exchanged(frames, groups, n, rows, width, sent)
    if not late:
        return smoothed(taps, stage, low, high, groups, 0, owned, col_tiles, 0, owned)
    tail = lax.slice(stage, (0, stage.shape[1] - REACH, 0, sent), stage.shape)
    head = lax.slice(stage, (0, 0, 0, sent), (n, REACH, rows, width))
    late_low = lax.ppermute(tail, "ta", [(i, i + 1) for i in range(groups - 1)])
    late_high = lax.ppermute(head, "ta", [(i + 1, i) for i in range(groups - 1)])
    out = smoothed(taps, stage, low, high, groups, 0, owned - late, col_tiles, 0, owned)
    return smoothed(taps, stage, late_low, late_high, groups, owned - late, late, col_tiles, owned - late, owned, out)


def solution(mesh):
    placed = (P("ta", "sa", None, None), P())
    return jax.shard_map(
        on_device, mesh=mesh, in_specs=placed, out_specs=P("sa", "ta", None, None), check_vma=False
    )
```

time: 1140 us -> 566 us (0.50)
  Pallas kernels: 0 us -> 526 us
  waiting for transfers between devices: 541 us -> 25 us
  blocking collectives: 369 us -> 0 us
  local copies, waits for them, and re-layouts: 131 us -> 7.16 us
  other arithmetic: 87.8 us -> 0 us
    pallas_call x0 -> x3, Pallas kernels: none -> 526 us  [the longest x1 479 us: exchanged(): pl.pallas_call(functools.partial(exchange_kernel, groups, n, rows, width,...]
    ppermute x2, waiting for transfers between devices: 541 us -> 25 us  [the longest x1 23.7 us: on_device(): lax.ppermute(head, 'ta', [(i + 1, i) for i in range(groups - 1)])]
    all_to_all x1 -> x0, blocking collectives: 369 us -> none  [on_device(): lax.all_to_all(pack_tiles(frames, readers), 'sa', split_axis=0, concat_ax...]
    add x1 -> x0, other arithmetic: 87.8 us -> none  [on_device(): total = total + taps[offset] * extended[:, offset:offset + steps]]
    transpose x2 -> x0, local copies, waits for them, and re-layouts: 60 us -> none  [the longest x1 31.8 us: unpack_tiles(): return received.transpose(0, 2, 3, 1, 4).reshape(owned, count, TS, TS)]
    unnamed x3 -> x2, local copies, waits for them, and re-layouts: 38 us -> 0.33 us
    slice x2 -> x1, local copies, waits for them, and re-layouts: 32.6 us -> 6.83 us  [on_device(): head = lax.slice(stage, (0, 0, 0, sent), (n, REACH, rows, width))]
  transfers between devices with their start and end apart: 2 -> 2, of which waited for: 2 -> 2; matrix products, arithmetic and copies ran while one was open for 0% -> 0% of each run, Pallas kernels for 0% -> 7%
where the time goes in v1:
time: 566 us
  Pallas kernels  526 us (93%)
  waiting for transfers between devices  25 us (4%)
  starting transfers between devices  7.65 us (1%)
  local copies, waits for them, and re-layouts  7.16 us (1%)
    pallas_call x1, Pallas kernels, exchanged(): pl.pallas_call(functools.partial(exchange_kernel, groups, n, rows, width,...  479 us
    pallas_call x2, Pallas kernels, smoothed(): pl.pallas_call(functools.partial(smooth_kernel, groups), grid=(count, spl...  47.1 us
    ppermute x1, waiting for transfers between devices, on_device(): lax.ppermute(head, 'ta', [(i + 1, i) for i in range(groups - 1)])  23.7 us
  transfers between devices with their start and end apart: 2, of which 2 were waited for; matrix products, arithmetic and copies ran while one was open for 0% of the time, Pallas kernels for 7%

profile of v1, /device:TPU:0, one launch (start us, length us, event | category | flops | bytes accessed | tf_op | source)
XLA Modules:
  0.0 566.1 jit_solution(12693771123057536673)
XLA Ops:
  0.0 479.1 %exchange.1 = (f32[8,4,64,4096]{3,2,1,0:T(8,128)}, f32[8,3,64,3584]{3,2,1,0:T(8,128)}, f32[8,3,64,3584]{3,2,1,0:T(8,128)}) custom-call(f32[4,1,512,4096]{3,2,1,0:T(8,128)} %frames.1), custom_call_target="tpu_custom_call" | custom-call | tf_op jit(solution)/shard_map/exchange/pallas_call | solution.py:119
  479.2 6.8 %fusion = (f32[8,3,64,512]{3,2,1,0:T(8,128)}, f32[8,3,64,512]{3,2,1,0:T(8,128)}) fusion(f32[8,4,64,4096]{3,2,1,0:T(8,128)} %get-tuple-element.8.stage), kind=kLoop, calls=%fused_computation | loop fusion | bytes 12582912 | tf_op jit(solution)/shard_map/slice | solution.py:206
  486.0 1.3 collective-permute-start.1
  487.3 6.4 %collective-permute-start = (f32[8,3,64,512]{3,2,1,0:T(8,128)}, f32[8,3,64,512]{3,2,1,0:T(8,128)}, u32[]{:S(2)}, u32[]{:S(2)}) collective-permute-start(f32[8,3,64,512]{3,2,1,0:T(8,128)} %get-tuple-element.12), channel_id=1, source_target_pairs={{0,8},{8,16},{16,24},{1,9},{9,17},{17,25},{2,10},{10,18},{18,26},{... | collective-permute-start | bytes 9437192 | tf_op jit(solution)/shard_map/ppermute | solution.py:207
  493.6 40.3 %smooth.2.rest_0_ = f32[8,4,512,512]{3,2,1,0:T(8,128)} custom-call(f32[7]{0:T(128)} %taps.3, f32[8,4,64,4096]{3,2,1,0:T(8,128)} %get-tuple-element.8.stage, f32[8,3,64,3584]{3,2,1,0:T(8,128)} %get-tuple-element.9.low, f32[8,3,64,3584]{3,2,1,0:T(8,128)} %get-tuple-element.10.high), custom_call_target="tpu_custom_call" | custom-call | flops 117440512 | bytes 102760448 | tf_op jit(solution)/shard_map/smooth/pallas_call | solution.py:179
  533.9 23.7 %collective-permute-done.1.high = f32[8,3,64,512]{3,2,1,0:T(8,128)S(1)} collective-permute-done((f32[8,3,64,512]{3,2,1,0:T(8,128)}, f32[8,3,64,512]{3,2,1,0:T(8,128)S(1)}, u32[]{:S(2)}, u32[]{:S(2)}) %collective-permute-start.1) | collective-permute-done | bytes 3145760 | tf_op jit(solution)/shard_map/ppermute | solution.py:208
  557.6 0.0 copy-start
  557.6 1.3 collective-permute-done.low
  558.9 0.3 copy-done
  559.2 6.8 %smooth.3 = f32[8,4,512,512]{3,2,1,0:T(8,128)} custom-call(f32[7]{0:T(128)} %taps.3, f32[8,4,64,4096]{3,2,1,0:T(8,128)} %get-tuple-element.8.stage, f32[8,3,64,512]{3,2,1,0:T(8,128)} %collective-permute-done.low, f32[8,3,64,512]{3,2,1,0:T(8,128)} %copy-done, f32[8,4,512,512]{3,2,1,0:T(8,128)} %smooth.2.rest_0_), custom_call_target="tpu_custom_call", output_to_operand_aliasing={{}: (4, {})} | custom-call | flops 16777216 | bytes 14680064 | tf_op jit(solution)/shard_map/smooth/pallas_call | solution.py:179
Async XLA Ops:
  486.0 71.6 %collective-permute-start.1 = (f32[8,3,64,512]{3,2,1,0:T(8,128)}, f32[8,3,64,512]{3,2,1,0:T(8,128)S(1)}, u32[]{:S(2)}, u32[]{:S(2)}) collective-permute-start(f32[8,3,64,512]{3,2,1,0:T(8,128)} %get-tuple-element.11), channel_id=1, source_target_pairs={{8,0},{16,8},{24,16},{9,1},{17,9},{25,17},{10,2},{18,10},{26,18},{... | collective-permute-start | bytes 9437192 | tf_op jit(solution)/shard_map/ppermute | solution.py:208
  487.3 71.6 %collective-permute-start = (f32[8,3,64,512]{3,2,1,0:T(8,128)}, f32[8,3,64,512]{3,2,1,0:T(8,128)}, u32[]{:S(2)}, u32[]{:S(2)}) collective-permute-start(f32[8,3,64,512]{3,2,1,0:T(8,128)} %get-tuple-element.12), channel_id=1, source_target_pairs={{0,8},{8,16},{16,24},{1,9},{9,17},{17,25},{2,10},{10,18},{18,26},{... | collective-permute-start | bytes 9437192 | tf_op jit(solution)/shard_map/ppermute | solution.py:207
  557.6 1.6 copy-start

commit v2 on v1

--- a/solution.py
+++ b/solution.py
@@ -10,6 +10,7 @@
 TS = 512
 REACH = 3
 LATE = 1
+LATE_SPAN = 256
 
 
 def partner(me, m, n, sign):
@@ -23,8 +24,13 @@
     return other
 
 
-def exchange_kernel(groups, n, rows, width, sent, frames, stage, low, high, own, own_sem,
-                    a_send, a_recv, up_send, up_recv, down_send, down_recv):
+def exchange_kernel(groups, n, rows, width, sent, frames, *refs):
+    late = sent < width
+    stage, low, high = refs[:3]
+    own, own_sem, a_send, a_recv, up_send, up_recv, down_send, down_recv = refs[-11 if late else -8:][:8]
+    if late:
+        head, tail = refs[3:5]
+        late_cells, late_load, late_store = refs[-3:]
     steps = frames.shape[0]
     group, me = lax.axis_index("ta"), lax.axis_index("sa")
     across = frames.shape[3] // width
@@ -59,17 +65,17 @@
         if m == 0:
             row = pl.ds(pl.multiple_of((me // across) * rows, 8), rows)
             col = pl.ds(pl.multiple_of((me % across) * width, TS), sent)
-            tail = frames.at[pl.ds(steps - REACH, REACH), 0, row, col]
-            head = frames.at[pl.ds(0, REACH), 0, row, col]
+            ending = frames.at[pl.ds(steps - REACH, REACH), 0, row, col]
+            opening = frames.at[pl.ds(0, REACH), 0, row, col]
         else:
-            tail = stage.at[source, pl.ds(steps - REACH, REACH), :, pl.ds(0, sent)]
-            head = stage.at[source, pl.ds(0, REACH), :, pl.ds(0, sent)]
+            ending = stage.at[source, pl.ds(steps - REACH, REACH), :, pl.ds(0, sent)]
+            opening = stage.at[source, pl.ds(0, REACH), :, pl.ds(0, sent)]
         if which == "up":
             return pltpu.make_async_remote_copy(
-                src_ref=tail, dst_ref=low.at[source],
+                src_ref=ending, dst_ref=low.at[source],
                 send_sem=up_send.at[m], recv_sem=up_recv.at[m], device_id={"ta": group + 1})
         return pltpu.make_async_remote_copy(
-            src_ref=head, dst_ref=high.at[source],
+            src_ref=opening, dst_ref=high.at[source],
             send_sem=down_send.at[m], recv_sem=down_recv.at[m], device_id={"ta": group - 1})
 
     def send_edges(m):
@@ -80,6 +86,26 @@
         @pl.when(has_prev)
         def _():
             edge_copy(m, "down").start()
+
+    def late_copies(m):
+        source = partner(me, m, n, -1)
+        return (
+            pltpu.make_async_copy(late_cells.at[m, pl.ds(steps - REACH, REACH)], tail.at[source], late_store.at[0, m]),
+            pltpu.make_async_copy(late_cells.at[m, pl.ds(0, REACH)], head.at[source], late_store.at[1, m]),
+        )
+
+    def take_late(m):
+        if m == 0:
+            row = pl.ds(pl.multiple_of((me // across) * rows, 8), rows)
+            col = pl.ds(pl.multiple_of((me % across) * width + sent, TS), width - sent)
+            cells = frames.at[:, 0, row, col]
+        else:
+            cells = stage.at[partner(me, m, n, -1), :, :, pl.ds(sent, width - sent)]
+        taken = pltpu.make_async_copy(cells, late_cells.at[m], late_load.at[m])
+        taken.start()
+        taken.wait()
+        for put in late_copies(m):
+            put.start()
 
     load = pltpu.make_async_copy(block_for(me), own, own_sem.at[0])
     load.start()
@@ -93,10 +119,18 @@
     load.wait()
     store = pltpu.make_async_copy(own, stage.at[me], own_sem.at[1])
     store.start()
+    if late:
+        take_late(0)
     for m in order:
         block_copy(m).wait_recv()
         send_edges(m)
+        if late:
+            take_late(m)
     store.wait()
+    if late:
+        for m in [0] + order:
+            for put in late_copies(m):
+                put.wait()
     for m in order:
         block_copy(m).wait_send()
     for m in [0] + order:
@@ -116,13 +150,17 @@
     any_space = pl.BlockSpec(memory_space=pl.ANY)
     edge = jax.ShapeDtypeStruct((n, REACH, rows, sent), jnp.float32)
     dma = pltpu.SemaphoreType.DMA((n,))
+    shapes = [jax.ShapeDtypeStruct((n, steps, rows, width), jnp.float32), edge, edge]
+    scratch = [pltpu.VMEM((steps, rows, width), jnp.float32), pltpu.SemaphoreType.DMA((2,))] + [dma] * 6
+    if sent < width:
+        shapes += [jax.ShapeDtypeStruct((n, REACH, rows, width - sent), jnp.float32)] * 2
+        scratch += [pltpu.VMEM((n, steps, rows, width - sent), jnp.float32), dma, pltpu.SemaphoreType.DMA((2, n))]
     return pl.pallas_call(
         functools.partial(exchange_kernel, groups, n, rows, width, sent),
-        out_shape=[jax.ShapeDtypeStruct((n, steps, rows, width), jnp.float32), edge, edge],
+        out_shape=shapes,
         in_specs=[any_space],
-        out_specs=[any_space] * 3,
-        scratch_shapes=[pltpu.VMEM((steps, rows, width), jnp.float32), pltpu.SemaphoreType.DMA((2,)),
-                        dma, dma, dma, dma, dma, dma],
+        out_specs=[any_space] * len(shapes),
+        scratch_shapes=scratch,
         compiler_params=pltpu.CompilerParams(collective_id=0, has_side_effects=True),
         name="exchange",
     )(frames)
@@ -156,10 +194,10 @@
             out[t, :, lanes] = woven[t]
 
 
-def smoothed(taps, stage, low, high, groups, start, count, col_tiles, edge_start, owned, into=None):
+def smoothed(taps, stage, low, high, groups, start, count, col_tiles, edge_start, owned, span, into=None):
     n, steps, rows, _ = stage.shape
     per_tile = TS // n
-    height = min(per_tile, max(8, 256 // n))
+    height = min(per_tile, max(8, span // n))
     splits = per_tile // height
 
     def source_map(shift):
@@ -199,15 +237,14 @@
     rows = max(1, owned // tile_cols) * (TS // n)
     late = LATE if owned == col_tiles and col_tiles > LATE else 0
     sent = width - late * TS
-    stage, low, high = exchanged(frames, groups, n, rows, width, sent)
+    stage, low, high, *edges = exchanged(frames, groups, n, rows, width, sent)
     if not late:
-        return smoothed(taps, stage, low, high, groups, 0, owned, col_tiles, 0, owned)
-    tail = lax.slice(stage, (0, stage.shape[1] - REACH, 0, sent), stage.shape)
-    head = lax.slice(stage, (0, 0, 0, sent), (n, REACH, rows, width))
+        return smoothed(taps, stage, low, high, groups, 0, owned, col_tiles, 0, owned, 256)
+    head, tail = edges
     late_low = lax.ppermute(tail, "ta", [(i, i + 1) for i in range(groups - 1)])
     late_high = lax.ppermute(head, "ta", [(i + 1, i) for i in range(groups - 1)])
-    out = smoothed(taps, stage, low, high, groups, 0, owned - late, col_tiles, 0, owned)
-    return smoothed(taps, stage, late_low, late_high, groups, owned - late, late, col_tiles, owned - late, owned, out)
+    out = smoothed(taps, stage, low, high, groups, 0, owned - late, col_tiles, 0, owned, 256)
+    return smoothed(taps, stage, late_low, late_high, groups, owned - late, late, col_tiles, owned - late, owned, LATE_SPAN, out)
 
 
 def solution(mesh):

time: 566 us -> 562 us (level)
  local copies, waits for them, and re-layouts: 7.16 us -> 0.01 us
    ppermute x1, waiting for transfers between devices: 1.28 us -> 25.6 us  [on_device(): late_low = lax.ppermute(tail, 'ta', [(i, i + 1) for i in range(groups - 1)])]
    ppermute x1, waiting for transfers between devices: 23.7 us -> 4.31 us  [on_device(): lax.ppermute(head, 'ta', [(i + 1, i) for i in range(groups - 1)])]
    slice x1 -> x0, local copies, waits for them, and re-layouts: 6.83 us -> none  [on_device(): head = lax.slice(stage, (0, 0, 0, sent), (n, REACH, rows, width))]
where the time goes in v2:
time: 562 us; the launch traced here: 561 us
  Pallas kernels  527 us (94%)
  waiting for transfers between devices  29.9 us (5%)
    pallas_call x1, Pallas kernels, exchanged(): pl.pallas_call(functools.partial(exchange_kernel, groups, n, rows, width,...  479 us
    pallas_call x2, Pallas kernels, smoothed(): pl.pallas_call(functools.partial(smooth_kernel, groups), grid=(count, spl...  47.1 us
    ppermute x1, waiting for transfers between devices, on_device(): late_low = lax.ppermute(tail, 'ta', [(i, i + 1) for i in range(groups - 1)])  25.6 us
  transfers between devices with their start and end apart: 2, of which 2 were waited for; matrix products, arithmetic and copies ran while one was open for 0% of the time, Pallas kernels for 7%

profile of v2, /device:TPU:0, one launch (start us, length us, event | category | flops | bytes accessed | tf_op | source)
XLA Modules:
  0.0 561.4 jit_solution(15877766665096604044)
XLA Ops:
  0.0 479.4 %exchange.1 = (f32[8,4,64,4096]{3,2,1,0:T(8,128)}, f32[8,3,64,3584]{3,2,1,0:T(8,128)}, f32[8,3,64,3584]{3,2,1,0:T(8,128)}, f32[8,3,64,512]{3,2,1,0:T(8,128)}, f32[8,3,64,512]{3,2,1,0:T(8,128)}) custom-call(f32[4,1,512,4096]{3,2,1,0:T(8,128)} %frames.1), custom_call_target="tpu_custom_call" | custom-call | tf_op jit(solution)/shard_map/exchange/pallas_call | solution.py:158
  479.4 3.7 collective-permute-start
  483.1 1.3 collective-permute-start.1
  484.4 40.3 %smooth.2.rest_0_ = f32[8,4,512,512]{3,2,1,0:T(8,128)} custom-call(f32[7]{0:T(128)} %taps.3, f32[8,4,64,4096]{3,2,1,0:T(8,128)} %get-tuple-element.10.stage, f32[8,3,64,3584]{3,2,1,0:T(8,128)} %get-tuple-element.13.low, f32[8,3,64,3584]{3,2,1,0:T(8,128)} %get-tuple-element.14.high), custom_call_target="tpu_custom_call" | custom-call | flops 117440512 | bytes 102760448 | tf_op jit(solution)/shard_map/smooth/pallas_call | solution.py:217
  524.7 25.6 %collective-permute-done.low = f32[8,3,64,512]{3,2,1,0:T(8,128)S(1)} collective-permute-done((f32[8,3,64,512]{3,2,1,0:T(8,128)}, f32[8,3,64,512]{3,2,1,0:T(8,128)S(1)}, u32[]{:S(2)}, u32[]{:S(2)}) %collective-permute-start) | collective-permute-done | bytes 3145760 | tf_op jit(solution)/shard_map/ppermute | solution.py:244
  550.2 0.0 copy-start
  550.2 4.3 collective-permute-done.1.high
  554.5 0.0 copy-done
  554.5 6.8 %smooth.3 = f32[8,4,512,512]{3,2,1,0:T(8,128)} custom-call(f32[7]{0:T(128)} %taps.3, f32[8,4,64,4096]{3,2,1,0:T(8,128)} %get-tuple-element.10.stage, f32[8,3,64,512]{3,2,1,0:T(8,128)} %copy-done, f32[8,3,64,512]{3,2,1,0:T(8,128)} %collective-permute-done.1.high, f32[8,4,512,512]{3,2,1,0:T(8,128)} %smooth.2.rest_0_), custom_call_target="tpu_custom_call", output_to_operand_aliasing={{}: (4, {})} | custom-call | flops 16777216 | bytes 14680064 | tf_op jit(solution)/shard_map/smooth/pallas_call | solution.py:217
Async XLA Ops:
  479.4 70.9 %collective-permute-start = (f32[8,3,64,512]{3,2,1,0:T(8,128)}, f32[8,3,64,512]{3,2,1,0:T(8,128)S(1)}, u32[]{:S(2)}, u32[]{:S(2)}) collective-permute-start(f32[8,3,64,512]{3,2,1,0:T(8,128)} %get-tuple-element.11), channel_id=1, source_target_pairs={{0,8},{8,16},{16,24},{1,9},{9,17},{17,25},{2,10},{10,18},{18,26},{... | collective-permute-start | bytes 9437192 | tf_op jit(solution)/shard_map/ppermute | solution.py:244
  483.1 71.5 %collective-permute-start.1 = (f32[8,3,64,512]{3,2,1,0:T(8,128)}, f32[8,3,64,512]{3,2,1,0:T(8,128)}, u32[]{:S(2)}, u32[]{:S(2)}) collective-permute-start(f32[8,3,64,512]{3,2,1,0:T(8,128)} %get-tuple-element.12), channel_id=1, source_target_pairs={{8,0},{16,8},{24,16},{9,1},{17,9},{25,17},{10,2},{18,10},{26,18},{... | collective-permute-start | bytes 9437192 | tf_op jit(solution)/shard_map/ppermute | solution.py:245
  550.2 4.3 copy-start
